TPU v7x, 128 devices: a whole 4x4x4 slice. The times are simulated.
128 devices in a mesh: gz: 4 (over x_lo, core), gy: 32 (over y, x_hi, z).
Axes of the slice: x: 4 (x_hi: 2, x_lo: 2; x = x_hi * 2 + x_lo), y: 4, z: 4, core: 2. Of those that a mesh axis runs over, the one named last changes fastest.
Arguments:
- distance: float32 [256, 512, 1024], P('gz', 'gy'), may hold values from 0 to 2
- parent: int32 [256, 512, 1024], P('gz', 'gy'), may hold values from 0 to 4095, as said below
- removed: int32 [4096], replicated, may hold values from 0 to 1
- occupied: int32 [256, 512, 1024], P('gz', 'gy'), may hold values 0 or 1
Outputs:
- lowered: float32 [256, 512, 1024], P('gz', 'gy')
- cleared_share: float32 [], replicated
Inputs may be any that keep to these rules, and one draw needn't show every extreme that they name: `parent`: an obstacle id.
All inputs are finite; a program needn't handle non-finite values. No bound on the sum of `occupied` on one device may be relied on, other than what follows from the above.
Results may differ from a plain program's by a relative error of at most 0.0003.
Values sent between devices are 32-bit elements; how exact they have to be, the bound alone decides.
A program may use at most 64 MiB of HBM per device.

v0:
```python
import functools

import jax
import jax.numpy as jnp
from jax import lax
from jax.sharding import Mesh
from jax.sharding import PartitionSpec as P

GZ = ("gz_0", "gz_1")
GZ_GY = ("gz_0", "gz_1", "gy_0", "gy_1", "gy_2")
GY = ("gy_0", "gy_1", "gy_2")


FAR = 1000000.0
VOXEL = 0.1
TRUNC = 2.0
LOW_IDS = 64
BLOCKS = 16


def padded_2(shard, sides, width):
    edges = {}
    for axis, dim in sides:
        size, length = (lax.axis_size(axis), shard.shape[dim])
        up = [(i, (i + 1) % size) for i in range(size)]
        last = lax.slice_in_dim(shard, length - width, length, axis=dim)
        first = lax.slice_in_dim(shard, 0, width, axis=dim)
        edges[dim] = (
            lax.ppermute(last, axis, up),
            lax.ppermute(first, axis, [(b, a) for a, b in up]),
        )
    done = []
    for _, dim in sides:
        low, high = edges[dim]
        around = [(width, width) if d in done else (0, 0) for d in range(shard.ndim)]
        shard = jnp.concatenate([jnp.pad(low, around), shard, jnp.pad(high, around)], axis=dim)
        done.append(dim)
    return shard


def by_axis(shard, axes):
    return functools.reduce(lax.psum, axes, shard)


def fence(field, width, slab_depth):
    planes = lax.iota(jnp.int32, field.shape[0]) + lax.axis_index(GZ) * slab_depth - width
    inside = (planes >= 0) & (planes < slab_depth * lax.axis_size(GZ))
    return jnp.where(inside[:, None, None], field, FAR)


def sweep(field):
    center = field[1:-1, 1:-1]
    nearest = jnp.minimum(field[2:, 1:-1], field[:-2, 1:-1])
    nearest = jnp.minimum(nearest, jnp.minimum(field[1:-1, 2:], field[1:-1, :-2]))
    far_col = jnp.full(center.shape[:2] + (1,), FAR, center.dtype)
    right = jnp.concatenate([center[:, :, 1:], far_col], 2)
    left = jnp.concatenate([far_col, center[:, :, :-1]], 2)
    nearest = jnp.minimum(nearest, jnp.minimum(left, right))
    return jnp.minimum(center, nearest + VOXEL)


def lookup_block(ids, table):
    high_count = table.shape[1]
    width = ids.shape[0]
    high_ids = ids // LOW_IDS
    low_ids = ids % LOW_IDS
    onehot = (lax.broadcasted_iota(jnp.int32, (high_count, width), 0) == high_ids[None, :]).astype(
        jnp.bfloat16
    )
    rows = jnp.dot(table, onehot, preferred_element_type=jnp.float32)
    picked = lax.broadcasted_iota(jnp.int32, (LOW_IDS, width), 0) == low_ids[None, :]
    return jnp.sum(jnp.where(picked, rows, 0.0), axis=0)


def on_device(distance, parent, removed, occupied):
    slab_depth = distance.shape[0]
    table = removed.reshape(-1, LOW_IDS).T.astype(jnp.bfloat16)
    blocked = parent.reshape(BLOCKS, -1)
    flagged = lax.map(lambda ids: lookup_block(ids, table), blocked).reshape(parent.shape)
    cleared = ((flagged > 0.5) & (occupied == 0)).astype(jnp.int32)
    raised = jnp.where(
        occupied == 1,
        jnp.zeros_like(distance),
        jnp.where(cleared == 1, jnp.full_like(distance, TRUNC), distance),
    )
    local_count = jnp.sum(cleared)
    field = raised
    for step in range(2):
        padded = padded_2(field, ((GZ, 0), (GY, 1)), 1)
        field = sweep(fence(padded, 1, slab_depth))
    count = by_axis(local_count, GZ_GY)
    total = (
        slab_depth * distance.shape[1] * distance.shape[2] * lax.axis_size(GZ) * lax.axis_size(GY)
    )
    share = jnp.asarray(count).astype(jnp.float32) * jnp.float32(100.0 / total)
    return (field, share)


def solution(mesh):
    torus = Mesh(mesh.devices.reshape(2, 2, 4, 2, 4), ("gz_0", "gz_1", "gy_0", "gy_1", "gy_2"))
    placed = (P(GZ, GY, None), P(GZ, GY, None), P(), P(GZ, GY, None))
    return jax.shard_map(
        on_device, mesh=torus, in_specs=placed, out_specs=(P(GZ, GY, None), P()), check_vma=False
    )
```

profile of v0, /device:TPU:1, one launch (start us, length us, event | category | flops | bytes accessed | tf_op | source)
XLA Modules:
  0.0 381.0 jit_solution(9333237715004989942)
XLA Ops:
  1.5 3.9 %reshape.20 = s32[16,65536]{1,0:T(8,128)} reshape(s32[64,16,1024]{2,1,0:T(8,128)} %param.7) | data formatting | bytes 8388608 | tf_op jit(solution)/shard_map/reshape | solution.py:78
  5.4 269.2 %while.12 = (s32[]{:T(128)}, f32[16,65536]{1,0:T(8,128)}, s32[16,65536]{1,0:T(8,128)}, bf16[64,64]{1,0:T(8,128)(2,1)S(1)}, s32[]{:T(128)}, /*index=5*/s32[]{:T(128)}) while((s32[]{:T(128)}, f32[16,65536]{1,0:T(8,128)}, s32[16,65536]{1,0:T(8,128)}, bf16[64,64]{1,0:T(8,128)(2,1)S(1)}, s32[]{:T(128)}, /*index=5*/s32[]{:T(128)}) %tuple.43), condition=%wide.region_2.3_spmd, body=%wide.region_0.2_spmd.sunk | while | flops 555089920 | bytes 2891865 | solution.py:79
  7.9 2.7 and_select_fusion.5
  10.6 5.6 %fusion.23 = f32[65536]{0:T(1024)S(1)} fusion(bf16[64,64]{1,0:T(8,128)(2,1)S(1)} %get-tuple-element.139, s32[65536]{0:T(1024)S(1)} %bitcast.23, s32[65536]{0:T(1024)S(1)} %bitcast.22), kind=kOutput, calls=%fused_computation.5.clone.1 | convolution fusion | flops 553582592 | bytes 794624 | tf_op jit(solution)/shard_map/while/body/eval_jaxpr/dot_general | solution.py:70
  16.3 6.0 %dynamic_update_slice.8 = f32[16,65536]{1,0:T(8,128)} dynamic-update-slice(f32[16,65536]{1,0:T(8,128)} %get-tuple-element.131, f32[1,65536]{1,0:T(1,128)S(1)} %bitcast.21, s32[]{:T(128)S(6)} %copy.24, s32[]{:T(128)} %constant.92.clone.1..sunk) | dynamic-update-slice | bytes 524292 | tf_op jit(solution)/shard_map/while/body/jit(dynamic_update_index_in_dim)/dynamic_update_slice | solution.py:79
  24.8 2.7 and_select_fusion.5
  27.5 5.6 %fusion.23 = f32[65536]{0:T(1024)S(1)} fusion(bf16[64,64]{1,0:T(8,128)(2,1)S(1)} %get-tuple-element.139, s32[65536]{0:T(1024)S(1)} %bitcast.23, s32[65536]{0:T(1024)S(1)} %bitcast.22), kind=kOutput, calls=%fused_computation.5.clone.1 | convolution fusion | flops 553582592 | bytes 794624 | tf_op jit(solution)/shard_map/while/body/eval_jaxpr/dot_general | solution.py:70
  33.1 6.0 %dynamic_update_slice.8 = f32[16,65536]{1,0:T(8,128)} dynamic-update-slice(f32[16,65536]{1,0:T(8,128)} %get-tuple-element.131, f32[1,65536]{1,0:T(1,128)S(1)} %bitcast.21, s32[]{:T(128)S(6)} %copy.24, s32[]{:T(128)} %constant.92.clone.1..sunk) | dynamic-update-slice | bytes 524292 | tf_op jit(solution)/shard_map/while/body/jit(dynamic_update_index_in_dim)/dynamic_update_slice | solution.py:79
  41.6 2.7 and_select_fusion.5
  44.3 5.6 %fusion.23 = f32[65536]{0:T(1024)S(1)} fusion(bf16[64,64]{1,0:T(8,128)(2,1)S(1)} %get-tuple-element.139, s32[65536]{0:T(1024)S(1)} %bitcast.23, s32[65536]{0:T(1024)S(1)} %bitcast.22), kind=kOutput, calls=%fused_computation.5.clone.1 | convolution fusion | flops 553582592 | bytes 794624 | tf_op jit(solution)/shard_map/while/body/eval_jaxpr/dot_general | solution.py:70
  49.9 6.0 %dynamic_update_slice.8 = f32[16,65536]{1,0:T(8,128)} dynamic-update-slice(f32[16,65536]{1,0:T(8,128)} %get-tuple-element.131, f32[1,65536]{1,0:T(1,128)S(1)} %bitcast.21, s32[]{:T(128)S(6)} %copy.24, s32[]{:T(128)} %constant.92.clone.1..sunk) | dynamic-update-slice | bytes 524292 | tf_op jit(solution)/shard_map/while/body/jit(dynamic_update_index_in_dim)/dynamic_update_slice | solution.py:79
  58.4 2.7 and_select_fusion.5
  61.1 5.6 %fusion.23 = f32[65536]{0:T(1024)S(1)} fusion(bf16[64,64]{1,0:T(8,128)(2,1)S(1)} %get-tuple-element.139, s32[65536]{0:T(1024)S(1)} %bitcast.23, s32[65536]{0:T(1024)S(1)} %bitcast.22), kind=kOutput, calls=%fused_computation.5.clone.1 | convolution fusion | flops 553582592 | bytes 794624 | tf_op jit(solution)/shard_map/while/body/eval_jaxpr/dot_general | solution.py:70
  66.7 6.0 %dynamic_update_slice.8 = f32[16,65536]{1,0:T(8,128)} dynamic-update-slice(f32[16,65536]{1,0:T(8,128)} %get-tuple-element.131, f32[1,65536]{1,0:T(1,128)S(1)} %bitcast.21, s32[]{:T(128)S(6)} %copy.24, s32[]{:T(128)} %constant.92.clone.1..sunk) | dynamic-update-slice | bytes 524292 | tf_op jit(solution)/shard_map/while/body/jit(dynamic_update_index_in_dim)/dynamic_update_slice | solution.py:79
  75.2 2.7 and_select_fusion.5
  77.9 5.6 %fusion.23 = f32[65536]{0:T(1024)S(1)} fusion(bf16[64,64]{1,0:T(8,128)(2,1)S(1)} %get-tuple-element.139, s32[65536]{0:T(1024)S(1)} %bitcast.23, s32[65536]{0:T(1024)S(1)} %bitcast.22), kind=kOutput, calls=%fused_computation.5.clone.1 | convolution fusion | flops 553582592 | bytes 794624 | tf_op jit(solution)/shard_map/while/body/eval_jaxpr/dot_general | solution.py:70
  83.6 6.0 %dynamic_update_slice.8 = f32[16,65536]{1,0:T(8,128)} dynamic-update-slice(f32[16,65536]{1,0:T(8,128)} %get-tuple-element.131, f32[1,65536]{1,0:T(1,128)S(1)} %bitcast.21, s32[]{:T(128)S(6)} %copy.24, s32[]{:T(128)} %constant.92.clone.1..sunk) | dynamic-update-slice | bytes 524292 | tf_op jit(solution)/shard_map/while/body/jit(dynamic_update_index_in_dim)/dynamic_update_slice | solution.py:79
  92.1 2.7 and_select_fusion.5
  94.8 5.6 %fusion.23 = f32[65536]{0:T(1024)S(1)} fusion(bf16[64,64]{1,0:T(8,128)(2,1)S(1)} %get-tuple-element.139, s32[65536]{0:T(1024)S(1)} %bitcast.23, s32[65536]{0:T(1024)S(1)} %bitcast.22), kind=kOutput, calls=%fused_computation.5.clone.1 | convolution fusion | flops 553582592 | bytes 794624 | tf_op jit(solution)/shard_map/while/body/eval_jaxpr/dot_general | solution.py:70
  100.4 6.0 %dynamic_update_slice.8 = f32[16,65536]{1,0:T(8,128)} dynamic-update-slice(f32[16,65536]{1,0:T(8,128)} %get-tuple-element.131, f32[1,65536]{1,0:T(1,128)S(1)} %bitcast.21, s32[]{:T(128)S(6)} %copy.24, s32[]{:T(128)} %constant.92.clone.1..sunk) | dynamic-update-slice | bytes 524292 | tf_op jit(solution)/shard_map/while/body/jit(dynamic_update_index_in_dim)/dynamic_update_slice | solution.py:79
  108.9 2.7 and_select_fusion.5
  111.6 5.6 %fusion.23 = f32[65536]{0:T(1024)S(1)} fusion(bf16[64,64]{1,0:T(8,128)(2,1)S(1)} %get-tuple-element.139, s32[65536]{0:T(1024)S(1)} %bitcast.23, s32[65536]{0:T(1024)S(1)} %bitcast.22), kind=kOutput, calls=%fused_computation.5.clone.1 | convolution fusion | flops 553582592 | bytes 794624 | tf_op jit(solution)/shard_map/while/body/eval_jaxpr/dot_general | solution.py:70
  117.2 6.0 %dynamic_update_slice.8 = f32[16,65536]{1,0:T(8,128)} dynamic-update-slice(f32[16,65536]{1,0:T(8,128)} %get-tuple-element.131, f32[1,65536]{1,0:T(1,128)S(1)} %bitcast.21, s32[]{:T(128)S(6)} %copy.24, s32[]{:T(128)} %constant.92.clone.1..sunk) | dynamic-update-slice | bytes 524292 | tf_op jit(solution)/shard_map/while/body/jit(dynamic_update_index_in_dim)/dynamic_update_slice | solution.py:79
  125.7 2.7 and_select_fusion.5
  128.4 5.6 %fusion.23 = f32[65536]{0:T(1024)S(1)} fusion(bf16[64,64]{1,0:T(8,128)(2,1)S(1)} %get-tuple-element.139, s32[65536]{0:T(1024)S(1)} %bitcast.23, s32[65536]{0:T(1024)S(1)} %bitcast.22), kind=kOutput, calls=%fused_computation.5.clone.1 | convolution fusion | flops 553582592 | bytes 794624 | tf_op jit(solution)/shard_map/while/body/eval_jaxpr/dot_general | solution.py:70
  134.0 6.0 %dynamic_update_slice.8 = f32[16,65536]{1,0:T(8,128)} dynamic-update-slice(f32[16,65536]{1,0:T(8,128)} %get-tuple-element.131, f32[1,65536]{1,0:T(1,128)S(1)} %bitcast.21, s32[]{:T(128)S(6)} %copy.24, s32[]{:T(128)} %constant.92.clone.1..sunk) | dynamic-update-slice | bytes 524292 | tf_op jit(solution)/shard_map/while/body/jit(dynamic_update_index_in_dim)/dynamic_update_slice | solution.py:79
  142.5 2.7 and_select_fusion.5
  145.2 5.6 %fusion.23 = f32[65536]{0:T(1024)S(1)} fusion(bf16[64,64]{1,0:T(8,128)(2,1)S(1)} %get-tuple-element.139, s32[65536]{0:T(1024)S(1)} %bitcast.23, s32[65536]{0:T(1024)S(1)} %bitcast.22), kind=kOutput, calls=%fused_computation.5.clone.1 | convolution fusion | flops 553582592 | bytes 794624 | tf_op jit(solution)/shard_map/while/body/eval_jaxpr/dot_general | solution.py:70
  150.9 6.0 %dynamic_update_slice.8 = f32[16,65536]{1,0:T(8,128)} dynamic-update-slice(f32[16,65536]{1,0:T(8,128)} %get-tuple-element.131, f32[1,65536]{1,0:T(1,128)S(1)} %bitcast.21, s32[]{:T(128)S(6)} %copy.24, s32[]{:T(128)} %constant.92.clone.1..sunk) | dynamic-update-slice | bytes 524292 | tf_op jit(solution)/shard_map/while/body/jit(dynamic_update_index_in_dim)/dynamic_update_slice | solution.py:79
  159.4 2.7 and_select_fusion.5
  162.1 5.6 %fusion.23 = f32[65536]{0:T(1024)S(1)} fusion(bf16[64,64]{1,0:T(8,128)(2,1)S(1)} %get-tuple-element.139, s32[65536]{0:T(1024)S(1)} %bitcast.23, s32[65536]{0:T(1024)S(1)} %bitcast.22), kind=kOutput, calls=%fused_computation.5.clone.1 | convolution fusion | flops 553582592 | bytes 794624 | tf_op jit(solution)/shard_map/while/body/eval_jaxpr/dot_general | solution.py:70
  167.7 6.0 %dynamic_update_slice.8 = f32[16,65536]{1,0:T(8,128)} dynamic-update-slice(f32[16,65536]{1,0:T(8,128)} %get-tuple-element.131, f32[1,65536]{1,0:T(1,128)S(1)} %bitcast.21, s32[]{:T(128)S(6)} %copy.24, s32[]{:T(128)} %constant.92.clone.1..sunk) | dynamic-update-slice | bytes 524292 | tf_op jit(solution)/shard_map/while/body/jit(dynamic_update_index_in_dim)/dynamic_update_slice | solution.py:79
  178.9 5.6 %fusion.23 = f32[65536]{0:T(1024)S(1)} fusion(bf16[64,64]{1,0:T(8,128)(2,1)S(1)} %get-tuple-element.139, s32[65536]{0:T(1024)S(1)} %bitcast.23, s32[65536]{0:T(1024)S(1)} %bitcast.22), kind=kOutput, calls=%fused_computation.5.clone.1 | convolution fusion | flops 553582592 | bytes 794624 | tf_op jit(solution)/shard_map/while/body/eval_jaxpr/dot_general | solution.py:70
  184.5 6.0 %dynamic_update_slice.8 = f32[16,65536]{1,0:T(8,128)} dynamic-update-slice(f32[16,65536]{1,0:T(8,128)} %get-tuple-element.131, f32[1,65536]{1,0:T(1,128)S(1)} %bitcast.21, s32[]{:T(128)S(6)} %copy.24, s32[]{:T(128)} %constant.92.clone.1..sunk) | dynamic-update-slice | bytes 524292 | tf_op jit(solution)/shard_map/while/body/jit(dynamic_update_index_in_dim)/dynamic_update_slice | solution.py:79
  195.7 5.6 %fusion.23 = f32[65536]{0:T(1024)S(1)} fusion(bf16[64,64]{1,0:T(8,128)(2,1)S(1)} %get-tuple-element.139, s32[65536]{0:T(1024)S(1)} %bitcast.23, s32[65536]{0:T(1024)S(1)} %bitcast.22), kind=kOutput, calls=%fused_computation.5.clone.1 | convolution fusion | flops 553582592 | bytes 794624 | tf_op jit(solution)/shard_map/while/body/eval_jaxpr/dot_general | solution.py:70
  201.3 6.0 %dynamic_update_slice.8 = f32[16,65536]{1,0:T(8,128)} dynamic-update-slice(f32[16,65536]{1,0:T(8,128)} %get-tuple-element.131, f32[1,65536]{1,0:T(1,128)S(1)} %bitcast.21, s32[]{:T(128)S(6)} %copy.24, s32[]{:T(128)} %constant.92.clone.1..sunk) | dynamic-update-slice | bytes 524292 | tf_op jit(solution)/shard_map/while/body/jit(dynamic_update_index_in_dim)/dynamic_update_slice | solution.py:79
  212.5 5.6 %fusion.23 = f32[65536]{0:T(1024)S(1)} fusion(bf16[64,64]{1,0:T(8,128)(2,1)S(1)} %get-tuple-element.139, s32[65536]{0:T(1024)S(1)} %bitcast.23, s32[65536]{0:T(1024)S(1)} %bitcast.22), kind=kOutput, calls=%fused_computation.5.clone.1 | convolution fusion | flops 553582592 | bytes 794624 | tf_op jit(solution)/shard_map/while/body/eval_jaxpr/dot_general | solution.py:70
  218.2 6.0 %dynamic_update_slice.8 = f32[16,65536]{1,0:T(8,128)} dynamic-update-slice(f32[16,65536]{1,0:T(8,128)} %get-tuple-element.131, f32[1,65536]{1,0:T(1,128)S(1)} %bitcast.21, s32[]{:T(128)S(6)} %copy.24, s32[]{:T(128)} %constant.92.clone.1..sunk) | dynamic-update-slice | bytes 524292 | tf_op jit(solution)/shard_map/while/body/jit(dynamic_update_index_in_dim)/dynamic_update_slice | solution.py:79
  226.7 2.7 and_select_fusion.5
  229.4 5.6 %fusion.23 = f32[65536]{0:T(1024)S(1)} fusion(bf16[64,64]{1,0:T(8,128)(2,1)S(1)} %get-tuple-element.139, s32[65536]{0:T(1024)S(1)} %bitcast.23, s32[65536]{0:T(1024)S(1)} %bitcast.22), kind=kOutput, calls=%fused_computation.5.clone.1 | convolution fusion | flops 553582592 | bytes 794624 | tf_op jit(solution)/shard_map/while/body/eval_jaxpr/dot_general | solution.py:70
  235.0 6.0 %dynamic_update_slice.8 = f32[16,65536]{1,0:T(8,128)} dynamic-update-slice(f32[16,65536]{1,0:T(8,128)} %get-tuple-element.131, f32[1,65536]{1,0:T(1,128)S(1)} %bitcast.21, s32[]{:T(128)S(6)} %copy.24, s32[]{:T(128)} %constant.92.clone.1..sunk) | dynamic-update-slice | bytes 524292 | tf_op jit(solution)/shard_map/while/body/jit(dynamic_update_index_in_dim)/dynamic_update_slice | solution.py:79
  243.5 2.7 and_select_fusion.5
  246.2 5.6 %fusion.23 = f32[65536]{0:T(1024)S(1)} fusion(bf16[64,64]{1,0:T(8,128)(2,1)S(1)} %get-tuple-element.139, s32[65536]{0:T(1024)S(1)} %bitcast.23, s32[65536]{0:T(1024)S(1)} %bitcast.22), kind=kOutput, calls=%fused_computation.5.clone.1 | convolution fusion | flops 553582592 | bytes 794624 | tf_op jit(solution)/shard_map/while/body/eval_jaxpr/dot_general | solution.py:70
  251.8 6.0 %dynamic_update_slice.8 = f32[16,65536]{1,0:T(8,128)} dynamic-update-slice(f32[16,65536]{1,0:T(8,128)} %get-tuple-element.131, f32[1,65536]{1,0:T(1,128)S(1)} %bitcast.21, s32[]{:T(128)S(6)} %copy.24, s32[]{:T(128)} %constant.92.clone.1..sunk) | dynamic-update-slice | bytes 524292 | tf_op jit(solution)/shard_map/while/body/jit(dynamic_update_index_in_dim)/dynamic_update_slice | solution.py:79
  263.0 5.6 %fusion.23 = f32[65536]{0:T(1024)S(1)} fusion(bf16[64,64]{1,0:T(8,128)(2,1)S(1)} %get-tuple-element.139, s32[65536]{0:T(1024)S(1)} %bitcast.23, s32[65536]{0:T(1024)S(1)} %bitcast.22), kind=kOutput, calls=%fused_computation.5.clone.1 | convolution fusion | flops 553582592 | bytes 794624 | tf_op jit(solution)/shard_map/while/body/eval_jaxpr/dot_general | solution.py:70
  268.6 6.0 %dynamic_update_slice.8 = f32[16,65536]{1,0:T(8,128)} dynamic-update-slice(f32[16,65536]{1,0:T(8,128)} %get-tuple-element.131, f32[1,65536]{1,0:T(1,128)S(1)} %bitcast.21, s32[]{:T(128)S(6)} %copy.24, s32[]{:T(128)} %constant.92.clone.1..sunk) | dynamic-update-slice | bytes 524292 | tf_op jit(solution)/shard_map/while/body/jit(dynamic_update_index_in_dim)/dynamic_update_slice | solution.py:79
  274.7 2.7 broadcast_compare_fusion
  278.5 4.7 %select_select_fusion = f32[64,16,1024]{2,1,0:T(8,128)S(1)} fusion(f32[64,16,1024]{2,1,0:T(8,128)} %param.6, s32[64,16,1024]{2,1,0:T(8,128)} %param.9, pred[64,16,1024]{2,1,0:T(8,128)(4,1)S(1)} %gt.11), kind=kLoop, calls=%fused_computation.33 | loop fusion | flops 7340032 | bytes 13631488 | tf_op jit(solution)/shard_map/jit(_where)/select_n | solution.py:81
  283.8 9.6 %collective-permute-start.3 = (f32[64,1,1024]{2,0,1:T(8,128)S(1)}, f32[64,1,1024]{2,0,1:T(8,128)S(1)}, u32[]{:S(2)}, u32[]{:S(2)}) collective-permute-start(f32[64,1,1024]{2,0,1:T(8,128)S(1)} %copy.15), channel_id=1, source_target_pairs={{1,0},{2,1},{3,2},{4,3},{5,4},{6,5},{7,6},{8,7},{9,8},{10,9},{11,1... | collective-permute-start | bytes 786440 | tf_op jit(solution)/shard_map/ppermute | solution.py:30
  294.8 3.5 collective-permute-done.3
  298.6 7.5 %collective-permute-done = f32[64,1,1024]{2,0,1:T(8,128)S(1)} collective-permute-done((f32[64,1,1024]{2,0,1:T(8,128)S(1)}, f32[64,1,1024]{2,0,1:T(8,128)S(1)}, u32[]{:S(2)}, u32[]{:S(2)}) %collective-permute-start) | collective-permute-done | bytes 262176 | tf_op jit(solution)/shard_map/ppermute | solution.py:29
  306.4 5.1 %fusion.4 = f32[66,18,1024]{2,1,0:T(8,128)S(1)} fusion(f32[64,1,1024]{2,1,0:T(1,128)S(1)} %copy.16, f32[64,1,1024]{2,1,0:T(1,128)S(1)} %copy.14, f32[1,16,1024]{2,1,0:T(8,128)S(1)} %collective-permute-done.2, f32[64,16,1024]{2,1,0:T(8,128)} %copy-done, f32[1,16,1024]{2,1,0:T(8,128)S(1)} %collective-permute-done.1, pred[66]{0:T(512)(128)(4,1)S(1)} %compare_and_fusion.1), kind=kLoop, calls=%fused_computation.15 | loop fusion | flops 10948608 | bytes 9715778 | tf_op jit(solution)/shard_map/jit(_where)/select_n | solution.py:48
  311.6 5.4 %fusion.14 = (f32[64,16,1023]{2,1,0:T(8,128)}, f32[64,16,1023]{2,1,0:T(8,128)}) fusion(f32[66,18,1024]{2,1,0:T(8,128)S(1)} %fusion.4), kind=kLoop, calls=%fused_computation.38 | loop fusion | bytes 16760832 | tf_op jit(solution)/shard_map/slice | solution.py:57
  317.0 6.5 %fusion.12 = f32[64,16,1024]{2,1,0:T(8,128)S(1)} fusion(f32[66,18,1024]{2,1,0:T(8,128)S(1)} %fusion.4, f32[64,16,1023]{2,1,0:T(8,128)} %get-tuple-element.86, f32[64,16,1023]{2,1,0:T(8,128)} %get-tuple-element.85), kind=kLoop, calls=%fused_computation.31 | loop fusion | flops 7340032 | bytes 33546240 | tf_op jit(solution)/shard_map/min | solution.py:59
  326.1 2.8 collective-permute-start.5
  330.5 3.9 %convert_reduce_fusion = s32[]{:T(128)} fusion(pred[64,16,1024]{2,1,0:T(8,128)(4,1)S(1)} %gt.11, s32[64,16,1024]{2,1,0:T(8,128)} %param.9), kind=kLoop, calls=%fused_computation.19 | loop fusion | flops 4194303 | bytes 5242884 | tf_op jit(solution)/shard_map/reduce_sum | solution.py:86
  334.4 3.8 psum.35
  338.2 5.3 %psum.36 = s32[]{:T(128)} all-reduce(s32[]{:T(128)} %psum.35), channel_id=1, replica_groups=mesh['gz_0'=2,'gz_1'=2,'gy_0'=4,'gy_1'=2,'gy_2'=4] {'gz_1'}, use_global_device_ids=true, to_apply=%region_5.6 | all-reduce | flops 1 | bytes 8 | tf_op jit(solution)/shard_map/psum | solution.py:42
  343.5 5.2 %psum.37 = s32[]{:T(128)} all-reduce(s32[]{:T(128)} %psum.36), channel_id=1, replica_groups=mesh['gz_0'=2,'gz_1'=2,'gy_0'=4,'gy_1'=2,'gy_2'=4] {'gy_0'}, use_global_device_ids=true, to_apply=%region_6.7 | all-reduce | flops 1 | bytes 8 | tf_op jit(solution)/shard_map/psum | solution.py:42
  348.8 5.2 %psum.38 = s32[]{:T(128)} all-reduce(s32[]{:T(128)} %psum.37), channel_id=1, replica_groups=mesh['gz_0'=2,'gz_1'=2,'gy_0'=4,'gy_1'=2,'gy_2'=4] {'gy_1'}, use_global_device_ids=true, to_apply=%region_7.8 | all-reduce | flops 1 | bytes 8 | tf_op jit(solution)/shard_map/psum | solution.py:42
  354.0 7.2 %psum.39 = s32[]{:T(128)} all-reduce(s32[]{:T(128)} %psum.38), channel_id=1, replica_groups=mesh['gz_0'=2,'gz_1'=2,'gy_0'=4,'gy_1'=2,'gy_2'=4] {'gy_2'}, use_global_device_ids=true, to_apply=%region_8.9 | all-reduce | flops 1 | bytes 8 | tf_op jit(solution)/shard_map/psum | solution.py:42
  362.5 5.1 %fusion.3 = f32[66,18,1024]{2,1,0:T(8,128)S(1)} fusion(f32[64,1,1024]{2,1,0:T(1,128)S(1)} %copy.20, f32[64,1,1024]{2,1,0:T(1,128)S(1)} %copy.18, f32[1,16,1024]{2,1,0:T(8,128)S(1)} %collective-permute-done.6, f32[64,16,1024]{2,1,0:T(8,128)} %copy-done.1, f32[1,16,1024]{2,1,0:T(8,128)S(1)} %collective-permute-done.5, pred[66]{0:T(512)(128)(4,1)S(1)} %compare_and_fusion.1), kind=kLoop, calls=%fused_computation.12 | loop fusion | flops 10948608 | bytes 9715778 | tf_op jit(solution)/shard_map/jit(_where)/select_n | solution.py:48
  367.6 4.7 %fusion.13 = (f32[64,16,1023]{2,1,0:T(8,128)S(1)}, f32[64,16,1023]{2,1,0:T(8,128)}) fusion(f32[66,18,1024]{2,1,0:T(8,128)S(1)} %fusion.3), kind=kLoop, calls=%fused_computation.37 | loop fusion | bytes 16760832 | tf_op jit(solution)/shard_map/slice | solution.py:57
  372.3 7.5 %fusion.8 = f32[64,16,1024]{2,1,0:T(8,128)} fusion(f32[66,18,1024]{2,1,0:T(8,128)S(1)} %fusion.3, f32[64,16,1023]{2,1,0:T(8,128)} %get-tuple-element.84, f32[64,16,1023]{2,1,0:T(8,128)S(1)} %get-tuple-element.83), kind=kLoop, calls=%fused_computation.25 | loop fusion | flops 7340032 | bytes 33546240 | tf_op jit(solution)/shard_map/min | solution.py:59
  (54 shorter events, 59.8 us)
Async XLA Ops:
  283.2 10.3 %copy-start = (f32[64,16,1024]{2,1,0:T(8,128)}, f32[64,16,1024]{2,1,0:T(8,128)S(1)}, u32[]{:S(2)}) copy-start(f32[64,16,1024]{2,1,0:T(8,128)S(1)} %select_select_fusion) | copy-start | bytes 12582916
  283.8 14.5 %collective-permute-start.3 = (f32[64,1,1024]{2,0,1:T(8,128)S(1)}, f32[64,1,1024]{2,0,1:T(8,128)S(1)}, u32[]{:S(2)}, u32[]{:S(2)}) collective-permute-start(f32[64,1,1024]{2,0,1:T(8,128)S(1)} %copy.15), channel_id=1, source_target_pairs={{1,0},{2,1},{3,2},{4,3},{5,4},{6,5},{7,6},{8,7},{9,8},{10,9},{11,1... | collective-permute-start | bytes 786440 | tf_op jit(solution)/shard_map/ppermute | solution.py:30
  293.4 12.7 %collective-permute-start = (f32[64,1,1024]{2,0,1:T(8,128)S(1)}, f32[64,1,1024]{2,0,1:T(8,128)S(1)}, u32[]{:S(2)}, u32[]{:S(2)}) collective-permute-start(f32[64,1,1024]{2,0,1:T(8,128)S(1)} %copy.13), channel_id=1, source_target_pairs={{0,1},{1,2},{2,3},{3,4},{4,5},{5,6},{6,7},{7,8},{8,9},{9,10},{10,1... | collective-permute-start | bytes 786440 | tf_op jit(solution)/shard_map/ppermute | solution.py:29
  293.5 12.9 %collective-permute-start.1 = (f32[1,16,1024]{2,1,0:T(8,128)S(1)}, f32[1,16,1024]{2,1,0:T(8,128)S(1)}, u32[]{:S(2)}, u32[]{:S(2)}) collective-permute-start(f32[1,16,1024]{2,1,0:T(8,128)S(1)} %get-tuple-element.91), channel_id=1, source_target_pairs={{0,32},{32,64},{64,96},{96,0},{1,33},{33,65},{65,97},{97,1},{2,34}... | collective-permute-start | bytes 196616 | tf_op jit(solution)/shard_map/ppermute | solution.py:29
  294.8 11.7 %collective-permute-start.2 = (f32[1,16,1024]{2,1,0:T(8,128)S(1)}, f32[1,16,1024]{2,1,0:T(8,128)S(1)}, u32[]{:S(2)}, u32[]{:S(2)}) collective-permute-start(f32[1,16,1024]{2,1,0:T(8,128)S(1)} %get-tuple-element.92), channel_id=1, source_target_pairs={{32,0},{64,32},{96,64},{0,96},{33,1},{65,33},{97,65},{1,97},{34,2}... | collective-permute-start | bytes 196616 | tf_op jit(solution)/shard_map/ppermute | solution.py:30
  323.5 2.0 copy-start.1
  326.1 36.4 %collective-permute-start.5 = (f32[1,16,1024]{2,1,0:T(8,128)S(1)}, f32[1,16,1024]{2,1,0:T(8,128)S(1)}, u32[]{:S(2)}, u32[]{:S(2)}) collective-permute-start(f32[1,16,1024]{2,1,0:T(8,128)S(1)} %get-tuple-element.87), channel_id=1, source_target_pairs={{0,32},{32,64},{64,96},{96,0},{1,33},{33,65},{65,97},{97,1},{2,34}... | collective-permute-start | bytes 196616 | tf_op jit(solution)/shard_map/ppermute | solution.py:29
  328.9 33.6 %collective-permute-start.6 = (f32[1,16,1024]{2,1,0:T(8,128)S(1)}, f32[1,16,1024]{2,1,0:T(8,128)S(1)}, u32[]{:S(2)}, u32[]{:S(2)}) collective-permute-start(f32[1,16,1024]{2,1,0:T(8,128)S(1)} %get-tuple-element.88), channel_id=1, source_target_pairs={{32,0},{64,32},{96,64},{0,96},{33,1},{65,33},{97,65},{1,97},{34,2}... | collective-permute-start | bytes 196616 | tf_op jit(solution)/shard_map/ppermute | solution.py:30
  329.0 32.9 %collective-permute-start.7 = (f32[64,1,1024]{2,0,1:T(8,128)S(1)}, f32[64,1,1024]{2,0,1:T(8,128)S(1)}, u32[]{:S(2)}, u32[]{:S(2)}) collective-permute-start(f32[64,1,1024]{2,0,1:T(8,128)S(1)} %copy.19), channel_id=1, source_target_pairs={{1,0},{2,1},{3,2},{4,3},{5,4},{6,5},{7,6},{8,7},{9,8},{10,9},{11,1... | collective-permute-start | bytes 786440 | tf_op jit(solution)/shard_map/ppermute | solution.py:30
  330.0 32.2 %collective-permute-start.4 = (f32[64,1,1024]{2,0,1:T(8,128)S(1)}, f32[64,1,1024]{2,0,1:T(8,128)S(1)}, u32[]{:S(2)}, u32[]{:S(2)}) collective-permute-start(f32[64,1,1024]{2,0,1:T(8,128)S(1)} %copy.17), channel_id=1, source_target_pairs={{0,1},{1,2},{2,3},{3,4},{4,5},{5,6},{6,7},{7,8},{8,9},{9,10},{10,1... | collective-permute-start | bytes 786440 | tf_op jit(solution)/shard_map/ppermute | solution.py:29
where the time goes:
time: 388 us; the launch traced here: 381 us
  other arithmetic  119 us (31%)
  local copies, waits for them, and re-layouts  116 us (30%)
  matrix products  89.7 us (23%)
  blocking collectives  26.8 us (7%)
  starting transfers between devices  15.2 us (4%)
  waiting for transfers between devices  11 us (3%)
    dynamic_update_slice x16, local copies, waits for them, and re-layouts, on_device(): lax.map(lambda ids: lookup_block(ids, table), blocked).reshape(parent.shape)  96.2 us
    dot_general x16, matrix products, lookup_block(): rows = jnp.dot(table, onehot, preferred_element_type=jnp.float32)  89.7 us
    select_n x16, other arithmetic, lookup_block(): high_ids = ids // LOW_IDS  43.4 us
    select_n x16, other arithmetic, lookup_block(): low_ids = ids % LOW_IDS  39.6 us
    psum x5, blocking collectives, by_axis(): return functools.reduce(lax.psum, axes, shard)  26.8 us
    min x2, other arithmetic, sweep(): return jnp.minimum(center, nearest + VOXEL)  14.1 us
    ppermute x4, starting transfers between devices, padded_2(): lax.ppermute(first, axis, [(b, a) for a, b in up])  10.6 us
    select_n x2, other arithmetic, fence(): return jnp.where(inside[:, None, None], field, FAR)  10.2 us
  transfers between devices with their start and end apart: 8, of which 2 were waited for; matrix products, arithmetic and copies ran while one was open for 1% of the time, Pallas kernels for 0%

commit v1 on v0

v1 whole, which is shorter than its diff:
```python
import functools

import jax
import jax.numpy as jnp
from jax import lax
from jax.experimental import pallas as pl
from jax.experimental.pallas import tpu as pltpu
from jax.sharding import PartitionSpec as P

MESH = pl.DeviceIdType.MESH
FAR = 1000000.0
VOXEL = 0.1
TRUNC = 2.0
Z, Y, X = 64, 16, 1024
XT = X // 128
PR = 24
RR = (Z + 2) * PR
CH = 8
NC = Z // CH
NGZ, NGY = 4, 32
SPLIT = (0,) + tuple(CH * c + CH + 1 for c in range(NC - 1)) + (Z,)


def lane_shifts(tiles, lane):
    far = jnp.full((8, 128), FAR, jnp.float32)
    up = [pltpu.roll(t, 127, 1) for t in tiles] + [far]
    down = [far] + [pltpu.roll(t, 1, 1) for t in tiles]
    right = [jnp.where(lane == 127, up[i + 1], up[i]) for i in range(len(tiles))]
    left = [jnp.where(lane == 0, down[i], down[i + 1]) for i in range(len(tiles))]
    return [jnp.minimum(a, b) for a, b in zip(right, left)]


def row(zp, y):
    return zp * PR + 8 + y


def kernel(
    dist_hbm, par_hbm, occ_hbm, rem_ref, out, share_ref,
    dist, par, occ, field, once, snd, hal, zhal, csnd, chal, tally, theirs,
    in_sem, ys_sem, yr_sem, zs_sem, zr_sem, cs_sem, cr_sem, ts_sem, tr_sem,
):
    gz, gy = lax.axis_index("gz"), lax.axis_index("gy")
    seg, zc = gy // 4, gy % 4
    lo, hi = (gz, (gy + NGY - 1) % NGY), (gz, (gy + 1) % NGY)
    below, above = (gz + NGZ - 1) % NGZ, (gz + 1) % NGZ
    diag = [[(g, t[1]) for t in (lo, hi)] for g in (below, above)]
    stage = [
        [(gz, seg * 4 + (zc + r) % 4) for r in range(1, 4)],
        [(gz, ((seg + r) % 8) * 4 + zc) for r in range(1, 8)],
        [((gz + r) % 4, gy) for r in range(1, 4)],
    ]
    first_slot = (0, 3, 10)
    friends = [lo, hi, (below, gy), (above, gy)] + diag[0] + diag[1] + stage[0] + stage[1] + stage[2]

    barrier = pltpu.get_barrier_semaphore()
    for friend in friends:
        pl.semaphore_signal(barrier, inc=1, device_id=friend, device_id_type=MESH)

    def fetch(c):
        a, n = SPLIT[c], SPLIT[c + 1] - SPLIT[c]
        return [
            pltpu.make_async_copy(src.at[pl.ds(a, n)], dst.at[pl.ds(a, n)], in_sem.at[i, c])
            for i, (src, dst) in enumerate(((dist_hbm, dist), (par_hbm, par), (occ_hbm, occ)))
        ]

    for c in range(NC):
        for copy in fetch(c):
            copy.start()

    lane = lax.broadcasted_iota(jnp.int32, (8, 128), 1)
    far_tile = jnp.full((8, 128), FAR, jnp.float32)

    bits = rem_ref[...] << lax.broadcasted_iota(jnp.int32, (32, 128), 0)
    words = jnp.broadcast_to(jnp.sum(bits, axis=0, keepdims=True), (8, 128))

    def pad_plane(zp, _):
        for xt in range(XT):
            base = pl.multiple_of(xt * RR + zp * PR, 8)
            field[pl.ds(base, 8), :] = far_tile
            once[pl.ds(base, 8), :] = far_tile
        return 0

    lax.fori_loop(0, Z + 2, pad_plane, 0)
    for xt in range(XT):
        for zp in (0, Z + 1):
            for half in (8, 16):
                field[pl.ds(xt * RR + zp * PR + half, 8), :] = far_tile
                once[pl.ds(xt * RR + zp * PR + half, 8), :] = far_tile
    for side in range(2):
        for plane in range(2):
            for xt in range(XT):
                zhal[side, plane, xt, pl.ds(0, 8), :] = far_tile
                zhal[side, plane, xt, pl.ds(24, 8), :] = far_tile

    def raise_plane(z, acc):
        for yt in range(2):
            for xt in range(XT):
                at = (z, pl.ds(yt * 8, 8), pl.ds(xt * 128, 128))
                ids, busy = par[at], occ[at]
                word = jnp.take_along_axis(words, ids & 127, axis=1, mode="promise_in_bounds")
                gone = lax.shift_right_logical(word, ids >> 7) & (1 - busy)
                raised = jnp.where(gone == 1, TRUNC, dist[at])
                raised = jnp.where(busy == 1, 0.0, raised)
                field[pl.ds(pl.multiple_of(xt * RR + (z + 1) * PR + 8 + yt * 8, 8), 8), :] = raised
                acc = acc + gone
        return acc

    def pack(c):
        first = c * CH + 1
        for side in range(2):
            y1, y2 = ((0, 1), (15, 14))[side]

            def rows(zp, y, xt):
                return field[pl.ds(xt * RR + row(zp, y), CH, stride=PR), :]

            near = [rows(first, y1, xt) for xt in range(XT)]
            around = lane_shifts(near, lane)
            for xt in range(XT):
                two = jnp.minimum(around[xt], rows(first, y2, xt))
                two = jnp.minimum(two, jnp.minimum(rows(first - 1, y1, xt), rows(first + 1, y1, xt)))
                snd[side, c, 0, xt] = jnp.minimum(near[xt] + VOXEL, two + VOXEL + VOXEL)
                snd[side, c, 1, xt] = near[xt] + VOXEL + VOXEL

    def y_copy(side, c):
        return pltpu.make_async_remote_copy(
            src_ref=snd.at[side, c], dst_ref=hal.at[1 - side, c],
            send_sem=ys_sem.at[side, c], recv_sem=yr_sem.at[1 - side, c],
            device_id=(lo, hi)[side], device_id_type=MESH,
        )

    def y_send(c):
        for side in (1, 0):
            y_copy(side, c).start()

    def z_copy(side, plane):
        zp = ((1, 2), (Z, Z - 1))[side][plane]
        return [
            pltpu.make_async_remote_copy(
                src_ref=field.at[pl.ds(xt * RR + row(zp, 0), 16)],
                dst_ref=zhal.at[1 - side, plane, xt, pl.ds(8, 16)],
                send_sem=zs_sem.at[side, plane, xt], recv_sem=zr_sem.at[1 - side, plane, xt],
                device_id=((below, gy), (above, gy))[side], device_id_type=MESH,
            )
            for xt in range(XT)
        ]

    def corner_copy(zs, ys):
        return pltpu.make_async_remote_copy(
            src_ref=csnd.at[zs, ys], dst_ref=chal.at[1 - zs, 1 - ys],
            send_sem=cs_sem.at[zs, ys], recv_sem=cr_sem.at[1 - zs, 1 - ys],
            device_id=diag[zs][ys], device_id_type=MESH,
        )

    def z_copies(side):
        return z_copy(side, 0) + z_copy(side, 1) + [corner_copy(side, 0), corner_copy(side, 1)]

    has = (gz > 0, gz < NGZ - 1)

    def z_send(side):
        for ys in range(2):
            csnd[side, ys] = field[pl.ds(row((1, Z)[side], (0, Y - 1)[ys]), 8, stride=RR), :]

        @pl.when(has[side])
        def _():
            for copy in z_copies(side):
                copy.start()

    def tally_copies(s):
        return [
            pltpu.make_async_remote_copy(
                src_ref=tally.at[s], dst_ref=theirs.at[first_slot[s] + r],
                send_sem=ts_sem.at[first_slot[s] + r], recv_sem=tr_sem.at[first_slot[s] + r],
                device_id=peer, device_id_type=MESH,
            )
            for r, peer in enumerate(stage[s])
        ]

    def tally_send(s, value):
        tally[s] = value
        for copy in tally_copies(s):
            copy.start()

    def tally_wait(s, value):
        for r, copy in enumerate(tally_copies(s)):
            copy.wait()
            value = value + theirs[first_slot[s] + r]
        return value

    def sweep_chunk(src, store, c):
        def plane(z, _):
            for yt in range(2):
                base = [xt * RR + (z + 1) * PR + 8 + yt * 8 for xt in range(XT)]
                here = [src[pl.ds(pl.multiple_of(b, 8), 8), :] for b in base]
                around = lane_shifts(here, lane)
                for xt in range(XT):
                    b = base[xt]
                    m = jnp.minimum(
                        src[pl.ds(pl.multiple_of(b - PR, 8), 8), :],
                        src[pl.ds(pl.multiple_of(b + PR, 8), 8), :],
                    )
                    m = jnp.minimum(m, jnp.minimum(src[pl.ds(b - 1, 8), :], src[pl.ds(b + 1, 8), :]))
                    m = jnp.minimum(m, around[xt])
                    store(z, yt, xt, jnp.minimum(here[xt], m + VOXEL))
            return 0

        lax.fori_loop(c * CH, (c + 1) * CH, plane, 0)

    def store_once(z, yt, xt, value):
        once[pl.ds(pl.multiple_of(xt * RR + (z + 1) * PR + 8 + yt * 8, 8), 8), :] = value

    def out_row(z, yt, xt):
        return ((z * 2 + yt) * XT + xt) * 8

    def store_out(z, yt, xt, value):
        out[pl.ds(pl.multiple_of(out_row(z, yt, xt), 8), 8), :] = value

    acc = jnp.zeros((8, 128), jnp.int32)
    for c in range(NC):
        for copy in fetch(c):
            copy.wait()
        acc = lax.fori_loop(SPLIT[c], SPLIT[c + 1], raise_plane, acc)
        pack(c)
        if c == 3:
            pl.semaphore_wait(barrier, len(friends))
            y_send(0)
            z_send(0)
        if c == 5:
            y_send(1)
    z_send(1)
    tally_send(0, acc)
    y_send(2)
    y_send(3)

    for c in range(NC):
        sweep_chunk(field, store_once, c)
        if c in (1, 3, 5, 7):
            y_send(4 + c // 2)
        if c == 5:
            acc = tally_wait(0, acc)
            tally_send(1, acc)
    for c in range(NC):
        sweep_chunk(once, store_out, c)
        if c == 3:
            acc = tally_wait(1, acc)
            tally_send(2, acc)

    for side in range(2):
        z0, z1 = ((0, 1), (Z - 1, Z - 2))[side]

        @pl.when(has[side])
        def _():
            for sent, came in zip(z_copies(side), z_copies(1 - side)):
                sent.wait_send()
                came.wait_recv()
            for yt in range(2):
                near = [zhal[side, 0, xt, pl.ds(8 + yt * 8, 8), :] for xt in range(XT)]
                around = lane_shifts(near, lane)
                for xt in range(XT):
                    two = jnp.minimum(around[xt], zhal[side, 1, xt, pl.ds(8 + yt * 8, 8), :])
                    two = jnp.minimum(
                        two,
                        jnp.minimum(
                            zhal[side, 0, xt, pl.ds(7 + yt * 8, 8), :],
                            zhal[side, 0, xt, pl.ds(9 + yt * 8, 8), :],
                        ),
                    )
                    add0 = jnp.minimum(near[xt] + VOXEL, two + VOXEL + VOXEL)
                    at0 = pl.ds(out_row(z0, yt, xt), 8)
                    out[at0, :] = jnp.minimum(out[at0, :], add0)
                    at1 = pl.ds(out_row(z1, yt, xt), 8)
                    out[at1, :] = jnp.minimum(out[at1, :], near[xt] + VOXEL + VOXEL)
            for ys in range(2):
                at = pl.ds(out_row(z0, ys, 0) + (0, 7)[ys], 8, stride=8)
                out[at, :] = jnp.minimum(out[at, :], chal[side, ys] + VOXEL + VOXEL)

    acc = tally_wait(2, acc)
    count = jnp.sum(acc)
    share_ref[0, 0] = count.astype(jnp.float32) * jnp.float32(100.0 / (NGZ * Z * NGY * Y * X))

    for c in range(NC):
        for side in range(2):
            y_copy(1 - side, c).wait()
            for which in range(2):
                y = ((0, 1), (15, 14))[side][which]
                for xt in range(XT):
                    at = pl.ds(out_row(c * CH, y // 8, xt) + y % 8, CH, stride=2 * XT * 8)
                    out[at, :] = jnp.minimum(out[at, :], hal[side, c, which, xt])


def on_device(distance, parent, removed, occupied):
    hbm = pl.BlockSpec(memory_space=pltpu.HBM)
    vmem = pl.BlockSpec(memory_space=pltpu.VMEM)
    dma = pltpu.SemaphoreType.DMA
    flat, share = pl.pallas_call(
        kernel,
        out_shape=(
            jax.ShapeDtypeStruct((Z * Y * XT, 128), jnp.float32),
            jax.ShapeDtypeStruct((1, 1), jnp.float32),
        ),
        in_specs=[hbm, hbm, hbm, vmem],
        out_specs=(vmem, pl.BlockSpec(memory_space=pltpu.SMEM)),
        scratch_shapes=[
            pltpu.VMEM((Z, Y, X), jnp.float32),
            pltpu.VMEM((Z, Y, X), jnp.int32),
            pltpu.VMEM((Z, Y, X), jnp.int32),
            pltpu.VMEM((XT * RR, 128), jnp.float32),
            pltpu.VMEM((XT * RR, 128), jnp.float32),
            pltpu.VMEM((2, NC, 2, XT, CH, 128), jnp.float32),
            pltpu.VMEM((2, NC, 2, XT, CH, 128), jnp.float32),
            pltpu.VMEM((2, 2, XT, 32, 128), jnp.float32),
            pltpu.VMEM((2, 2, 8, 128), jnp.float32),
            pltpu.VMEM((2, 2, 8, 128), jnp.float32),
            pltpu.VMEM((3, 8, 128), jnp.int32),
            pltpu.VMEM((13, 8, 128), jnp.int32),
            dma((3, NC)),
            dma((2, NC)),
            dma((2, NC)),
            dma((2, 2, XT)),
            dma((2, 2, XT)),
            dma((2, 2)),
            dma((2, 2)),
            dma((13,)),
            dma((13,)),
        ],
        compiler_params=pltpu.CompilerParams(
            collective_id=0, has_side_effects=True, vmem_limit_bytes=57 * 2**20
        ),
    )(distance, parent, occupied, removed.reshape(32, 128))
    lowered = flat.reshape(Z, 2, XT, 8, 128).transpose(0, 1, 3, 2, 4).reshape(Z, Y, X)
    return lowered, share.reshape(())


def solution(mesh):
    block = P("gz", "gy", None)
    return jax.shard_map(
        on_device, mesh=mesh, in_specs=(block, block, P(), block), out_specs=(block, P()), check_vma=False
    )
```

time: 388 us -> 43.2 us (0.11); the launches traced: 381 us -> 43 us
  other arithmetic: 119 us -> 0 us
  local copies, waits for them, and re-layouts: 116 us -> 4.79 us
  matrix products: 89.7 us -> 0 us
  Pallas kernels: 0 us -> 35.8 us
  blocking collectives: 26.8 us -> 0 us
  starting transfers between devices: 15.2 us -> 0 us
  waiting for transfers between devices: 11 us -> 0 us
    select_n x35 -> x0, other arithmetic: 98 us -> none  [the longest x16 43.4 us: lookup_block(): high_ids = ids // LOW_IDS]
    dynamic_update_slice x16 -> x0, local copies, waits for them, and re-layouts: 96.2 us -> none  [on_device(): lax.map(lambda ids: lookup_block(ids, table), blocked).reshape(parent.shape)]
    dot_general x16 -> x0, matrix products: 89.7 us -> none  [lookup_block(): rows = jnp.dot(table, onehot, preferred_element_type=jnp.float32)]
    pallas_call x0 -> x1, Pallas kernels: none -> 35.8 us  [on_device(): pl.pallas_call(kernel, out_shape=(jax.ShapeDtypeStruct((Z * Y * XT, 128),...]
    psum x5 -> x0, blocking collectives: 26.8 us -> none  [by_axis(): return functools.reduce(lax.psum, axes, shard)]
    ppermute x8 -> x0, starting transfers between devices: 15.2 us -> none  [the longest x4 10.6 us: padded_2(): lax.ppermute(first, axis, [(b, a) for a, b in up])]
    min x2 -> x0, other arithmetic: 14.1 us -> none  [sweep(): return jnp.minimum(center, nearest + VOXEL)]
    slice x10 -> x0, local copies, waits for them, and re-layouts: 11.4 us -> none  [the longest x2 10.1 us: sweep(): left = jnp.concatenate([far_col, center[:, :, :-1]], 2)]
  transfers between devices with their start and end apart: 8 -> 0, of which waited for: 2 -> 0; matrix products, arithmetic and copies ran while one was open for 1% -> 0% of each run, Pallas kernels for 0% -> 0%
where the time goes in v1:
time: 43.2 us; the launch traced here: 43 us
  Pallas kernels  35.8 us (83%)
  local copies, waits for them, and re-layouts  4.79 us (11%)
  between operations  2.38 us (6%)
    pallas_call x1, Pallas kernels, on_device(): pl.pallas_call(kernel, out_shape=(jax.ShapeDtypeStruct((Z * Y * XT, 128),...  35.8 us
    unnamed x1, local copies, waits for them, and re-layouts  4.79 us

profile of v1, /device:TPU:1, one launch (start us, length us, event | category | flops | bytes accessed | tf_op | source)
XLA Modules:
  0.0 43.0 jit_solution(10348179815390102977)
XLA Ops:
  0.6 35.8 %shard_map.59 = (f32[8192,128]{1,0:T(8,128)}, f32[1,1]{1,0:T(1,128)}) custom-call(f32[64,16,1024]{2,1,0:T(8,128)} %dist_hbm.1, s32[64,16,1024]{2,1,0:T(8,128)} %par_hbm.1, s32[64,16,1024]{2,1,0:T(8,128)} %occ_hbm.1, s32[32,128]{1,0:T(8,128)} %bitcast.8), custom_call_target="tpu_custom_call" | custom-call | tf_op jit(solution)/shard_map/pallas_call | solution.py:294
  36.4 4.8 %copy.8 = f32[64,16,1024]{2,1,0:T(8,128)} copy(f32[64,16,1024]{2,1,0:T(8,128)} %bitcast.7) | data formatting | bytes 8388608

commit v2 on v1

--- a/solution.py
+++ b/solution.py
@@ -18,6 +18,10 @@
 CH = 8
 NC = Z // CH
 NGZ, NGY = 4, 32
+WAIT_AT = 2
+EARLY = ((), (), (0, 1), (2,), (), (), (), (3,))
+UNITS = (0, 7, 1, 2, 3, 4, 5, 6)
+READY = ((0,), (), (1,), (2,), (3,), (4,), (5,), (6, 7))
 SPLIT = (0,) + tuple(CH * c + CH + 1 for c in range(NC - 1)) + (Z,)
 
 
@@ -30,20 +34,33 @@
     return [jnp.minimum(a, b) for a, b in zip(right, left)]
 
 
+def lane_gather(table, index):
+    dims = lax.GatherDimensionNumbers(
+        offset_dims=(),
+        collapsed_slice_dims=(1,),
+        start_index_map=(1,),
+        operand_batching_dims=(0,),
+        start_indices_batching_dims=(0,),
+    )
+    mode = lax.GatherScatterMode.PROMISE_IN_BOUNDS
+    return lax.gather(table, index[..., None], dims, (1, 1), mode=mode)
+
+
 def row(zp, y):
     return zp * PR + 8 + y
 
 
 def kernel(
-    dist_hbm, par_hbm, occ_hbm, rem_ref, out, share_ref,
-    dist, par, occ, field, once, snd, hal, zhal, csnd, chal, tally, theirs,
-    in_sem, ys_sem, yr_sem, zs_sem, zr_sem, cs_sem, cr_sem, ts_sem, tr_sem,
+    dist_hbm, par_hbm, occ_hbm, rem_hbm, out, share_ref,
+    dist, par, occ, field, once, snd, hal, zhal, csnd, chal, tally, theirs, rem,
+    rem_sem, in_sem, ys_sem, yr_sem, zs_sem, zr_sem, cs_sem, cr_sem, ts_sem, tr_sem,
 ):
     gz, gy = lax.axis_index("gz"), lax.axis_index("gy")
-    seg, zc = gy // 4, gy % 4
+    zc = gy % 4
     lo, hi = (gz, (gy + NGY - 1) % NGY), (gz, (gy + 1) % NGY)
     below, above = (gz + NGZ - 1) % NGZ, (gz + 1) % NGZ
     diag = [[(g, t[1]) for t in (lo, hi)] for g in (below, above)]
+    seg = gy // 4
     stage = [
         [(gz, seg * 4 + (zc + r) % 4) for r in range(1, 4)],
         [(gz, ((seg + r) % 8) * 4 + zc) for r in range(1, 8)],
@@ -56,6 +73,9 @@
     for friend in friends:
         pl.semaphore_signal(barrier, inc=1, device_id=friend, device_id_type=MESH)
 
+    fetch_removed = pltpu.make_async_copy(rem_hbm, rem, rem_sem)
+    fetch_removed.start()
+
     def fetch(c):
         a, n = SPLIT[c], SPLIT[c + 1] - SPLIT[c]
         return [
@@ -63,14 +83,15 @@
             for i, (src, dst) in enumerate(((dist_hbm, dist), (par_hbm, par), (occ_hbm, occ)))
         ]
 
-    for c in range(NC):
+    for c in UNITS:
         for copy in fetch(c):
             copy.start()
 
     lane = lax.broadcasted_iota(jnp.int32, (8, 128), 1)
     far_tile = jnp.full((8, 128), FAR, jnp.float32)
 
-    bits = rem_ref[...] << lax.broadcasted_iota(jnp.int32, (32, 128), 0)
+    fetch_removed.wait()
+    bits = rem[...] << lax.broadcasted_iota(jnp.int32, (32, 128), 0)
     words = jnp.broadcast_to(jnp.sum(bits, axis=0, keepdims=True), (8, 128))
 
     def pad_plane(zp, _):
@@ -97,7 +118,7 @@
             for xt in range(XT):
                 at = (z, pl.ds(yt * 8, 8), pl.ds(xt * 128, 128))
                 ids, busy = par[at], occ[at]
-                word = jnp.take_along_axis(words, ids & 127, axis=1, mode="promise_in_bounds")
+                word = lane_gather(words, ids & 127)
                 gone = lax.shift_right_logical(word, ids >> 7) & (1 - busy)
                 raised = jnp.where(gone == 1, TRUNC, dist[at])
                 raised = jnp.where(busy == 1, 0.0, raised)
@@ -152,17 +173,23 @@
         )
 
     def z_copies(side):
-        return z_copy(side, 0) + z_copy(side, 1) + [corner_copy(side, 0), corner_copy(side, 1)]
+        return z_copy(side, 0) + z_copy(side, 1)
+
+    def corners(side):
+        return [corner_copy(side, 0), corner_copy(side, 1)]
 
     has = (gz > 0, gz < NGZ - 1)
 
     def z_send(side):
-        for ys in range(2):
-            csnd[side, ys] = field[pl.ds(row((1, Z)[side], (0, Y - 1)[ys]), 8, stride=RR), :]
-
         @pl.when(has[side])
         def _():
             for copy in z_copies(side):
+                copy.start()
+
+    def corner_send(side):
+        @pl.when(has[side])
+        def _():
+            for copy in corners(side):
                 copy.start()
 
     def tally_copies(s):
@@ -203,7 +230,7 @@
                     store(z, yt, xt, jnp.minimum(here[xt], m + VOXEL))
             return 0
 
-        lax.fori_loop(c * CH, (c + 1) * CH, plane, 0)
+        lax.fori_loop(c * CH, (c + 1) * CH, plane, 0, unroll=8)
 
     def store_once(z, yt, xt, value):
         once[pl.ds(pl.multiple_of(xt * RR + (z + 1) * PR + 8 + yt * 8, 8), 8), :] = value
@@ -215,41 +242,47 @@
         out[pl.ds(pl.multiple_of(out_row(z, yt, xt), 8), 8), :] = value
 
     acc = jnp.zeros((8, 128), jnp.int32)
-    for c in range(NC):
-        for copy in fetch(c):
+    for turn, u in enumerate(UNITS):
+        for copy in fetch(u):
             copy.wait()
-        acc = lax.fori_loop(SPLIT[c], SPLIT[c + 1], raise_plane, acc)
-        pack(c)
-        if c == 3:
+        acc = lax.fori_loop(SPLIT[u], SPLIT[u + 1], raise_plane, acc, unroll=8)
+        if turn == 1:
+            for zs in range(2):
+                for ys in range(2):
+                    csnd[zs, ys] = field[pl.ds(row((1, Z)[zs], (0, Y - 1)[ys]), 8, stride=RR), :]
+        for c in READY[turn]:
+            pack(c)
+        if turn == WAIT_AT:
             pl.semaphore_wait(barrier, len(friends))
-            y_send(0)
-            z_send(0)
-        if c == 5:
-            y_send(1)
-    z_send(1)
+            corner_send(0)
+            corner_send(1)
+        if turn >= WAIT_AT:
+            for c in EARLY[turn]:
+                y_send(c)
     tally_send(0, acc)
-    y_send(2)
-    y_send(3)
+    y_send(4)
 
     for c in range(NC):
         sweep_chunk(field, store_once, c)
-        if c in (1, 3, 5, 7):
-            y_send(4 + c // 2)
         if c == 5:
-            acc = tally_wait(0, acc)
-            tally_send(1, acc)
+            y_send(5)
     for c in range(NC):
         sweep_chunk(once, store_out, c)
-        if c == 3:
-            acc = tally_wait(1, acc)
-            tally_send(2, acc)
+        if c == 2:
+            y_send(6)
+        if c == 6:
+            y_send(7)
+            z_send(0)
+            z_send(1)
+    acc = tally_wait(0, acc)
+    tally_send(1, acc)
 
     for side in range(2):
         z0, z1 = ((0, 1), (Z - 1, Z - 2))[side]
 
         @pl.when(has[side])
         def _():
-            for sent, came in zip(z_copies(side), z_copies(1 - side)):
+            for sent, came in zip(z_copies(side) + corners(side), z_copies(1 - side) + corners(1 - side)):
                 sent.wait_send()
                 came.wait_recv()
             for yt in range(2):
@@ -273,10 +306,6 @@
                 at = pl.ds(out_row(z0, ys, 0) + (0, 7)[ys], 8, stride=8)
                 out[at, :] = jnp.minimum(out[at, :], chal[side, ys] + VOXEL + VOXEL)
 
-    acc = tally_wait(2, acc)
-    count = jnp.sum(acc)
-    share_ref[0, 0] = count.astype(jnp.float32) * jnp.float32(100.0 / (NGZ * Z * NGY * Y * X))
-
     for c in range(NC):
         for side in range(2):
             y_copy(1 - side, c).wait()
@@ -285,6 +314,13 @@
                 for xt in range(XT):
                     at = pl.ds(out_row(c * CH, y // 8, xt) + y % 8, CH, stride=2 * XT * 8)
                     out[at, :] = jnp.minimum(out[at, :], hal[side, c, which, xt])
+        if c == 5:
+            acc = tally_wait(1, acc)
+            tally_send(2, acc)
+
+    acc = tally_wait(2, acc)
+    count = jnp.sum(acc)
+    share_ref[0, 0] = count.astype(jnp.float32) * jnp.float32(100.0 / (NGZ * Z * NGY * Y * X))
 
 
 def on_device(distance, parent, removed, occupied):
@@ -297,7 +333,7 @@
             jax.ShapeDtypeStruct((Z * Y * XT, 128), jnp.float32),
             jax.ShapeDtypeStruct((1, 1), jnp.float32),
         ),
-        in_specs=[hbm, hbm, hbm, vmem],
+        in_specs=[hbm, hbm, hbm, hbm],
         out_specs=(vmem, pl.BlockSpec(memory_space=pltpu.SMEM)),
         scratch_shapes=[
             pltpu.VMEM((Z, Y, X), jnp.float32),
@@ -312,6 +348,8 @@
             pltpu.VMEM((2, 2, 8, 128), jnp.float32),
             pltpu.VMEM((3, 8, 128), jnp.int32),
             pltpu.VMEM((13, 8, 128), jnp.int32),
+            pltpu.VMEM((32, 128), jnp.int32),
+            dma,
             dma((3, NC)),
             dma((2, NC)),
             dma((2, NC)),
@@ -323,7 +361,7 @@
             dma((13,)),
         ],
         compiler_params=pltpu.CompilerParams(
-            collective_id=0, has_side_effects=True, vmem_limit_bytes=57 * 2**20
+            collective_id=0, has_side_effects=True, vmem_limit_bytes=48 * 2**20
         ),
     )(distance, parent, occupied, removed.reshape(32, 128))
     lowered = flat.reshape(Z, 2, XT, 8, 128).transpose(0, 1, 3, 2, 4).reshape(Z, Y, X)

time: 43.2 us -> 36.2 us (0.84)
  Pallas kernels: 35.8 us -> 30.9 us
  local copies, waits for them, and re-layouts: 4.79 us -> 2.73 us
    pallas_call x1, Pallas kernels: 35.8 us -> 30.9 us  [on_device(): pl.pallas_call(kernel, out_shape=(jax.ShapeDtypeStruct((Z * Y * XT, 128),...]
    unnamed x1 -> x3, local copies, waits for them, and re-layouts: 4.79 us -> 2.73 us
where the time goes in v2:
time: 36.2 us; the launch traced here: 36 us
  Pallas kernels  30.9 us (85%)
  local copies, waits for them, and re-layouts  2.73 us (8%)
  between operations  2.41 us (7%)
    pallas_call x1, Pallas kernels, on_device(): pl.pallas_call(kernel, out_shape=(jax.ShapeDtypeStruct((Z * Y * XT, 128),...  30.9 us
    unnamed x3, local copies, waits for them, and re-layouts  2.73 us

profile of v2, /device:TPU:1, one launch (start us, length us, event | category | flops | bytes accessed | tf_op | source)
XLA Modules:
  0.0 36.0 jit_solution(15149373964627596665)
XLA Ops:
  0.6 0.0 copy-start
  0.6 0.7 %copy-done = s32[4096]{0:T(1024)S(1)} copy-done((s32[4096]{0:T(1024)S(1)}, s32[4096]{0:T(1024)}, u32[]{:S(2)}) %copy-start) | copy-done | bytes 16408
  1.3 30.9 %shard_map.59 = (f32[8192,128]{1,0:T(8,128)S(1)}, f32[1,1]{1,0:T(1,128)}) custom-call(f32[64,16,1024]{2,1,0:T(8,128)} %dist_hbm.1, s32[64,16,1024]{2,1,0:T(8,128)} %par_hbm.1, s32[64,16,1024]{2,1,0:T(8,128)} %occ_hbm.1, s32[32,128]{1,0:T(8,128)S(1)} %bitcast.8), custom_call_target="tpu_custom_call" | custom-call | tf_op jit(solution)/shard_map/pallas_call | solution.py:330
  32.2 2.0 %copy.8 = f32[64,16,1024]{2,1,0:T(8,128)} copy(f32[64,16,1024]{2,1,0:T(8,128)S(1)} %bitcast.7) | data formatting | bytes 8388608
Async XLA Ops:
  0.6 0.7 %copy-start = (s32[4096]{0:T(1024)S(1)}, s32[4096]{0:T(1024)}, u32[]{:S(2)}) copy-start(s32[4096]{0:T(1024)} %param.6) | copy-start | bytes 49156

commit v3 on v2

--- a/solution.py
+++ b/solution.py
@@ -18,10 +18,11 @@
 CH = 8
 NC = Z // CH
 NGZ, NGY = 4, 32
-WAIT_AT = 2
-EARLY = ((), (), (0, 1), (2,), (), (), (), (3,))
-UNITS = (0, 7, 1, 2, 3, 4, 5, 6)
-READY = ((0,), (), (1,), (2,), (3,), (4,), (5,), (6, 7))
+WAIT_AT = 1
+UNITS = (0, 7, 6, 1, 2, 3, 4, 5)
+READY = ((0,), (), (7,), (1,), (2,), (3,), (4,), (5, 6))
+EARLY = ((), (0,), (7,), (1,), (2,), (), (), ())
+ORDER = (0, 7, 1, 2, 3, 4, 5, 6)
 SPLIT = (0,) + tuple(CH * c + CH + 1 for c in range(NC - 1)) + (Z,)
 
 
@@ -59,15 +60,14 @@
     zc = gy % 4
     lo, hi = (gz, (gy + NGY - 1) % NGY), (gz, (gy + 1) % NGY)
     below, above = (gz + NGZ - 1) % NGZ, (gz + 1) % NGZ
-    diag = [[(g, t[1]) for t in (lo, hi)] for g in (below, above)]
-    seg = gy // 4
+    yc, half = gy // 8, (gy // 4) % 2
     stage = [
-        [(gz, seg * 4 + (zc + r) % 4) for r in range(1, 4)],
-        [(gz, ((seg + r) % 8) * 4 + zc) for r in range(1, 8)],
-        [((gz + r) % 4, gy) for r in range(1, 4)],
+        [((gz + r) % 4, (yc * 2 + (half + h) % 2) * 4 + zc) for h in range(2) for r in range(4) if h or r],
+        [(gz, (gy // 4) * 4 + (zc + r) % 4) for r in range(1, 4)],
+        [(gz, (((yc + r) % 4) * 2 + half) * 4 + zc) for r in range(1, 4)],
     ]
-    first_slot = (0, 3, 10)
-    friends = [lo, hi, (below, gy), (above, gy)] + diag[0] + diag[1] + stage[0] + stage[1] + stage[2]
+    first_slot = (0, 7, 10)
+    friends = [lo, hi, (below, gy), (above, gy)] + stage[0] + stage[1] + stage[2]
 
     barrier = pltpu.get_barrier_semaphore()
     for friend in friends:
@@ -167,9 +167,9 @@
 
     def corner_copy(zs, ys):
         return pltpu.make_async_remote_copy(
-            src_ref=csnd.at[zs, ys], dst_ref=chal.at[1 - zs, 1 - ys],
-            send_sem=cs_sem.at[zs, ys], recv_sem=cr_sem.at[1 - zs, 1 - ys],
-            device_id=diag[zs][ys], device_id_type=MESH,
+            src_ref=csnd.at[zs, ys], dst_ref=chal.at[1 - zs, ys],
+            send_sem=cs_sem.at[zs, ys], recv_sem=cr_sem.at[1 - zs, ys],
+            device_id=((below, gy), (above, gy))[zs], device_id_type=MESH,
         )
 
     def z_copies(side):
@@ -187,6 +187,11 @@
                 copy.start()
 
     def corner_send(side):
+        for ys in range(2):
+            for xt in range(XT):
+                edge = hal[ys, (0, NC - 1)[side], 1, xt, pl.ds((0, CH - 1)[side], 1), :]
+                csnd[side, ys, pl.ds(xt, 1), :] = edge
+
         @pl.when(has[side])
         def _():
             for copy in corners(side):
@@ -246,34 +251,42 @@
         for copy in fetch(u):
             copy.wait()
         acc = lax.fori_loop(SPLIT[u], SPLIT[u + 1], raise_plane, acc, unroll=8)
-        if turn == 1:
-            for zs in range(2):
-                for ys in range(2):
-                    csnd[zs, ys] = field[pl.ds(row((1, Z)[zs], (0, Y - 1)[ys]), 8, stride=RR), :]
         for c in READY[turn]:
             pack(c)
         if turn == WAIT_AT:
             pl.semaphore_wait(barrier, len(friends))
-            corner_send(0)
-            corner_send(1)
         if turn >= WAIT_AT:
             for c in EARLY[turn]:
                 y_send(c)
     tally_send(0, acc)
+    y_send(3)
     y_send(4)
 
     for c in range(NC):
         sweep_chunk(field, store_once, c)
-        if c == 5:
+        if c == 3:
             y_send(5)
+        if c == 7:
+            y_send(6)
     for c in range(NC):
         sweep_chunk(once, store_out, c)
-        if c == 2:
-            y_send(6)
         if c == 6:
-            y_send(7)
             z_send(0)
             z_send(1)
+
+    def y_add(c):
+        for side in range(2):
+            y_copy(1 - side, c).wait()
+            for which in range(2):
+                y = ((0, 1), (15, 14))[side][which]
+                for xt in range(XT):
+                    at = pl.ds(out_row(c * CH, y // 8, xt) + y % 8, CH, stride=2 * XT * 8)
+                    out[at, :] = jnp.minimum(out[at, :], hal[side, c, which, xt])
+
+    for c in ORDER[:2]:
+        y_add(c)
+    corner_send(0)
+    corner_send(1)
     acc = tally_wait(0, acc)
     tally_send(1, acc)
 
@@ -304,17 +317,11 @@
                     out[at1, :] = jnp.minimum(out[at1, :], near[xt] + VOXEL + VOXEL)
             for ys in range(2):
                 at = pl.ds(out_row(z0, ys, 0) + (0, 7)[ys], 8, stride=8)
-                out[at, :] = jnp.minimum(out[at, :], chal[side, ys] + VOXEL + VOXEL)
-
-    for c in range(NC):
-        for side in range(2):
-            y_copy(1 - side, c).wait()
-            for which in range(2):
-                y = ((0, 1), (15, 14))[side][which]
-                for xt in range(XT):
-                    at = pl.ds(out_row(c * CH, y // 8, xt) + y % 8, CH, stride=2 * XT * 8)
-                    out[at, :] = jnp.minimum(out[at, :], hal[side, c, which, xt])
-        if c == 5:
+                out[at, :] = jnp.minimum(out[at, :], chal[side, ys])
+
+    for c in ORDER[2:]:
+        y_add(c)
+        if c == 4:
             acc = tally_wait(1, acc)
             tally_send(2, acc)
 

time: 36.2 us -> 33.7 us (0.931)
  Pallas kernels: 30.9 us -> 28.3 us
    pallas_call x1, Pallas kernels: 30.9 us -> 28.3 us  [on_device(): pl.pallas_call(kernel, out_shape=(jax.ShapeDtypeStruct((Z * Y * XT, 128),...]
where the time goes in v3:
time: 33.7 us; the launch traced here: 33.5 us
  Pallas kernels  28.3 us (84%)
  local copies, waits for them, and re-layouts  2.73 us (8%)
  between operations  2.41 us (7%)
    pallas_call x1, Pallas kernels, on_device(): pl.pallas_call(kernel, out_shape=(jax.ShapeDtypeStruct((Z * Y * XT, 128),...  28.3 us
    unnamed x3, local copies, waits for them, and re-layouts  2.73 us

profile of v3, /device:TPU:1, one launch (start us, length us, event | category | flops | bytes accessed | tf_op | source)
XLA Modules:
  0.0 33.5 jit_solution(9602428509585130802)
XLA Ops:
  0.6 0.0 copy-start
  0.6 0.7 %copy-done = s32[4096]{0:T(1024)S(1)} copy-done((s32[4096]{0:T(1024)S(1)}, s32[4096]{0:T(1024)}, u32[]{:S(2)}) %copy-start) | copy-done | bytes 16408
  1.3 28.3 %shard_map.59 = (f32[8192,128]{1,0:T(8,128)S(1)}, f32[1,1]{1,0:T(1,128)}) custom-call(f32[64,16,1024]{2,1,0:T(8,128)} %dist_hbm.1, s32[64,16,1024]{2,1,0:T(8,128)} %par_hbm.1, s32[64,16,1024]{2,1,0:T(8,128)} %occ_hbm.1, s32[32,128]{1,0:T(8,128)S(1)} %bitcast.8), custom_call_target="tpu_custom_call" | custom-call | tf_op jit(solution)/shard_map/pallas_call | solution.py:337
  29.7 2.0 %copy.8 = f32[64,16,1024]{2,1,0:T(8,128)} copy(f32[64,16,1024]{2,1,0:T(8,128)S(1)} %bitcast.7) | data formatting | bytes 8388608
Async XLA Ops:
  0.6 0.7 %copy-start = (s32[4096]{0:T(1024)S(1)}, s32[4096]{0:T(1024)}, u32[]{:S(2)}) copy-start(s32[4096]{0:T(1024)} %param.6) | copy-start | bytes 49156

commit v4 on v3

--- a/solution.py
+++ b/solution.py
@@ -52,9 +52,9 @@
 
 
 def kernel(
-    dist_hbm, par_hbm, occ_hbm, rem_hbm, out, share_ref,
-    dist, par, occ, field, once, snd, hal, zhal, csnd, chal, tally, theirs, rem,
-    rem_sem, in_sem, ys_sem, yr_sem, zs_sem, zr_sem, cs_sem, cr_sem, ts_sem, tr_sem,
+    dist_hbm, par_hbm, occ_hbm, rem_ref, out, share_ref,
+    dist, par, occ, field, once, snd, hal, zhal, csnd, chal, tally, theirs,
+    in_sem, ys_sem, yr_sem, zs_sem, zr_sem, cs_sem, cr_sem, ts_sem, tr_sem,
 ):
     gz, gy = lax.axis_index("gz"), lax.axis_index("gy")
     zc = gy % 4
@@ -73,9 +73,6 @@
     for friend in friends:
         pl.semaphore_signal(barrier, inc=1, device_id=friend, device_id_type=MESH)
 
-    fetch_removed = pltpu.make_async_copy(rem_hbm, rem, rem_sem)
-    fetch_removed.start()
-
     def fetch(c):
         a, n = SPLIT[c], SPLIT[c + 1] - SPLIT[c]
         return [
@@ -90,8 +87,7 @@
     lane = lax.broadcasted_iota(jnp.int32, (8, 128), 1)
     far_tile = jnp.full((8, 128), FAR, jnp.float32)
 
-    fetch_removed.wait()
-    bits = rem[...] << lax.broadcasted_iota(jnp.int32, (32, 128), 0)
+    bits = rem_ref[...] << lax.broadcasted_iota(jnp.int32, (32, 128), 0)
     words = jnp.broadcast_to(jnp.sum(bits, axis=0, keepdims=True), (8, 128))
 
     def pad_plane(zp, _):
@@ -283,12 +279,18 @@
                     at = pl.ds(out_row(c * CH, y // 8, xt) + y % 8, CH, stride=2 * XT * 8)
                     out[at, :] = jnp.minimum(out[at, :], hal[side, c, which, xt])
 
-    for c in ORDER[:2]:
-        y_add(c)
+    y_add(ORDER[0])
+    acc = tally_wait(0, acc)
+    tally_send(1, acc)
+    y_add(ORDER[1])
     corner_send(0)
     corner_send(1)
-    acc = tally_wait(0, acc)
-    tally_send(1, acc)
+
+    for c in ORDER[2:]:
+        y_add(c)
+        if c == 2:
+            acc = tally_wait(1, acc)
+            tally_send(2, acc)
 
     for side in range(2):
         z0, z1 = ((0, 1), (Z - 1, Z - 2))[side]
@@ -319,12 +321,6 @@
                 at = pl.ds(out_row(z0, ys, 0) + (0, 7)[ys], 8, stride=8)
                 out[at, :] = jnp.minimum(out[at, :], chal[side, ys])
 
-    for c in ORDER[2:]:
-        y_add(c)
-        if c == 4:
-            acc = tally_wait(1, acc)
-            tally_send(2, acc)
-
     acc = tally_wait(2, acc)
     count = jnp.sum(acc)
     share_ref[0, 0] = count.astype(jnp.float32) * jnp.float32(100.0 / (NGZ * Z * NGY * Y * X))
@@ -340,7 +336,7 @@
             jax.ShapeDtypeStruct((Z * Y * XT, 128), jnp.float32),
             jax.ShapeDtypeStruct((1, 1), jnp.float32),
         ),
-        in_specs=[hbm, hbm, hbm, hbm],
+        in_specs=[hbm, hbm, hbm, vmem],
         out_specs=(vmem, pl.BlockSpec(memory_space=pltpu.SMEM)),
         scratch_shapes=[
             pltpu.VMEM((Z, Y, X), jnp.float32),
@@ -355,8 +351,6 @@
             pltpu.VMEM((2, 2, 8, 128), jnp.float32),
             pltpu.VMEM((3, 8, 128), jnp.int32),
             pltpu.VMEM((13, 8, 128), jnp.int32),
-            pltpu.VMEM((32, 128), jnp.int32),
-            dma,
             dma((3, NC)),
             dma((2, NC)),
             dma((2, NC)),

time: 33.7 us -> 32.7 us (0.970)
  the two profiles are of different devices: /device:TPU:1 before, /device:TPU:0 now
where the time goes in v4:
time: 32.7 us; the launch traced here: 32.5 us
  Pallas kernels  27.4 us (84%)
  local copies, waits for them, and re-layouts  2.73 us (8%)
  between operations  2.41 us (7%)
    pallas_call x1, Pallas kernels, on_device(): pl.pallas_call(kernel, out_shape=(jax.ShapeDtypeStruct((Z * Y * XT, 128),...  27.4 us
    unnamed x3, local copies, waits for them, and re-layouts  2.73 us

profile of v4, /device:TPU:0, one launch (start us, length us, event | category | flops | bytes accessed | tf_op | source)
XLA Modules:
  0.0 32.5 jit_solution(3380213844401652806)
XLA Ops:
  0.6 0.0 copy-start
  0.6 0.7 %copy-done = s32[4096]{0:T(1024)S(1)} copy-done((s32[4096]{0:T(1024)S(1)}, s32[4096]{0:T(1024)}, u32[]{:S(2)}) %copy-start) | copy-done | bytes 16408
  1.3 27.4 %shard_map.59 = (f32[8192,128]{1,0:T(8,128)S(1)}, f32[1,1]{1,0:T(1,128)}) custom-call(f32[64,16,1024]{2,1,0:T(8,128)} %dist_hbm.1, s32[64,16,1024]{2,1,0:T(8,128)} %par_hbm.1, s32[64,16,1024]{2,1,0:T(8,128)} %occ_hbm.1, s32[32,128]{1,0:T(8,128)S(1)} %bitcast.8), custom_call_target="tpu_custom_call" | custom-call | tf_op jit(solution)/shard_map/pallas_call | solution.py:333
  28.7 2.0 %copy.8 = f32[64,16,1024]{2,1,0:T(8,128)} copy(f32[64,16,1024]{2,1,0:T(8,128)S(1)} %bitcast.7) | data formatting | bytes 8388608
Async XLA Ops:
  0.6 0.7 %copy-start = (s32[4096]{0:T(1024)S(1)}, s32[4096]{0:T(1024)}, u32[]{:S(2)}) copy-start(s32[4096]{0:T(1024)} %param.6) | copy-start | bytes 49156
